TPU v7x, 32 devices: a 4x4x1 block of a 4x4x8 slice. The times are simulated.
32 devices in a mesh: dp: 1 (over z), tp: 32 (over y, x, core).
Axes of the slice: x: 4, y: 4, z: 1, core: 2. Of those that a mesh axis runs over, the one named last changes fastest.
The devices are a block of a 4x4x8 slice.
Arguments:
- token_ids: int32 [4096], P('dp')
- emb_table: bfloat16 [51200, 2560], P('tp')
- norm_gain: bfloat16 [2560], replicated
- w_in: bfloat16 [2560, 10240], P(None, 'tp')
- w_out: bfloat16 [10240, 2560], P('tp')
- d_out: bfloat16 [4096, 2560], P(('dp', 'tp'))
Outputs:
- output 1: bfloat16 [4096, 2560], P(('dp', 'tp'))
- output 2: float32 [51200, 2560], P(('dp', 'tp'))
- output 3: float32 [2560, 10240], P('dp', 'tp')
- output 4: float32 [10240, 2560], P(('dp', 'tp'))
All inputs are finite; a program needn't handle non-finite values.
Results may differ from a plain program's by a relative error of at most 0.00843216.
Values are sent between devices in bfloat16 or wider.
A program may use at most 768 MiB of HBM per device.

v0:
```python
import jax
import jax.numpy as jnp
from jax import lax
from jax.sharding import PartitionSpec as P

EPS = 1e-6


def solution(mesh):
    def shard_step(token_ids, emb_table, norm_gain, w_in, w_out, d_out):
        shard_rank = lax.axis_index("tp")
        vocab_local = emb_table.shape[0]
        local_ids = token_ids - shard_rank * vocab_local
        is_owned = (local_ids >= 0) & (local_ids < vocab_local)
        table_rows = jnp.take(emb_table, jnp.where(is_owned, local_ids, 0), axis=0)
        lookup_part = jnp.where(is_owned[:, None], table_rows, jnp.zeros((), table_rows.dtype))
        embedded = lax.psum_scatter(lookup_part, "tp", scatter_dimension=0, tiled=True)
        embedded_f32 = embedded.astype(jnp.float32)
        inv_rms = lax.rsqrt(jnp.mean(embedded_f32 * embedded_f32, axis=-1, keepdims=True) + EPS)
        gain_f32 = norm_gain.astype(jnp.float32)
        normed_local = (embedded_f32 * inv_rms * gain_f32).astype(jnp.bfloat16)
        normed = lax.all_gather(normed_local, "tp", axis=0, tiled=True)
        pre_act = jnp.dot(normed, w_in, preferred_element_type=jnp.float32).astype(jnp.bfloat16)
        act_f32, gelu_vjp = jax.vjp(jax.nn.gelu, pre_act.astype(jnp.float32))
        hidden = act_f32.astype(jnp.bfloat16)
        mlp_part = jnp.dot(hidden, w_out, preferred_element_type=jnp.float32)
        mlp_out = lax.psum_scatter(mlp_part, "tp", scatter_dimension=0, tiled=True)
        block_out = (embedded_f32 + mlp_out).astype(jnp.bfloat16)

        d_out_full = lax.all_gather(d_out, "tp", axis=0, tiled=True)
        d_hidden = lax.dot_general(d_out_full, w_out, (((1,), (1,)), ((), ())), preferred_element_type=jnp.float32).astype(jnp.bfloat16)
        d_w_out = lax.dot_general(hidden, d_out_full, (((0,), (0,)), ((), ())), preferred_element_type=jnp.float32)
        (d_pre_f32,) = gelu_vjp(d_hidden.astype(jnp.float32))
        d_pre = d_pre_f32.astype(jnp.bfloat16)
        d_w_in = lax.dot_general(normed, d_pre, (((0,), (0,)), ((), ())), preferred_element_type=jnp.float32)
        d_norm_part = lax.dot_general(d_pre, w_in, (((1,), (1,)), ((), ())), preferred_element_type=jnp.float32)
        d_normed = lax.psum_scatter(d_norm_part, "tp", scatter_dimension=0, tiled=True)
        d_scaled = d_normed * gain_f32
        row_proj = jnp.mean(d_scaled * embedded_f32, axis=-1, keepdims=True)
        d_emb = (d_out.astype(jnp.float32) + inv_rms * (d_scaled - embedded_f32 * inv_rms * inv_rms * row_proj)).astype(jnp.bfloat16)
        d_emb_full = lax.all_gather(d_emb, "tp", axis=0, tiled=True)
        target_rows = jnp.where(is_owned, local_ids, vocab_local)
        d_table = jax.ops.segment_sum(d_emb_full.astype(jnp.float32), target_rows, num_segments=vocab_local)
        return block_out, d_table, d_w_in, d_w_out

    return jax.shard_map(
        shard_step,
        mesh=mesh,
        in_specs=(P("dp"), P("tp", None), P(None), P(None, "tp"), P("tp", None), P(("dp", "tp"), None)),
        out_specs=(P(("dp", "tp"), None), P(("dp", "tp"), None), P("dp", "tp"), P(("dp", "tp"), None)),
        check_vma=False,
    )
```

profile of v0, /device:TPU:97, one launch (start us, length us, event | category | flops | bytes accessed | tf_op | source)
XLA Modules:
  0.0 913.4 jit_solution(17561797535860798434)
XLA Ops:
  7.2 0.0 copy-start
  7.2 0.1 reduce-scatter.4.cloned.1.call-start
  7.3 0.8 compare_and_fusion.1
  8.1 1.3 subtract_select_fusion
  9.4 42.0 %gather_fusion = bf16[4096,2560]{1,0:T(8,128)(2,1)} fusion(bf16[1600,2560]{1,0:T(8,128)(2,1)} %param.7, s32[4096]{0:T(1024)S(1)} %get-tuple-element.7), kind=kCustom, calls=%fused_computation | custom fusion | bytes 41959424 | tf_op jit(solution)/shard_map/jit(_take)/gather | solution.py:15
  51.5 18.6 %select_select_fusion = bf16[4096,2560]{1,0:T(8,128)(2,1)} fusion(bf16[4096,2560]{1,0:T(8,128)(2,1)} %gather_fusion, pred[4096]{0:T(1024)(128)(4,1)S(1)} %get-tuple-element.9, pred[4096]{0:T(1024)(128)(4,1)S(1)} %get-tuple-element.8), kind=kLoop, calls=%fused_computation.4 | loop fusion | flops 20971520 | bytes 41951232 | tf_op jit(solution)/shard_map/jit(_where)/select_n | solution.py:16
  70.1 0.0 copy-start.7
  70.1 0.1 reduce-scatter.4.cloned.1.call-update
  70.1 0.1 all-gather.4.cloned.1.call-start
  70.2 0.6 copy-done.7
  70.8 122.7 %reduce-scatter.4.cloned.1.call-done = bf16[128,2560]{1,0:T(8,128)(2,1)} async-done(((bf16[4096,2560]{1,0:T(8,128)(2,1)}), bf16[128,2560]{1,0:T(8,128)(2,1)}) %reduce-scatter.4.cloned.1.call-update) | async-done | bytes 655376 | tf_op jit(solution)/shard_map/reduce_scatter | solution.py:17
  193.5 1.3 fusion.22
  194.8 2.1 fusion.16
  196.9 0.1 all-gather.4.cloned.1.call-update
  197.0 0.1 all-gather.6.cloned.1.call-start
  197.1 0.7 all-gather.6.cloned.1.call-update
  197.8 0.0 copy-start.6
  197.8 0.2 reduce-scatter.8.cloned.1.call-start
  198.0 77.1 %all-gather.4.cloned.1.call-done = bf16[4096,2560]{1,0:T(8,128)(2,1)} async-done(((bf16[128,2560]{1,0:T(8,128)(2,1)}), bf16[4096,2560]{1,0:T(8,128)(2,1)}) %all-gather.4.cloned.1.call-update) | async-done | bytes 20971536 | tf_op jit(solution)/shard_map/all_gather | solution.py:22
  275.2 0.0 copy-done
  275.2 13.0 %convolution_convert_fusion.1 = bf16[4096,320]{0,1:T(8,128)(2,1)} fusion(bf16[4096,2560]{1,0:T(8,128)(2,1)} %all-gather.4.cloned.1.call-done, bf16[2560,320]{0,1:T(8,128)(2,1)S(1)} %copy-done), kind=kOutput, calls=%fused_computation.14 | convolution fusion | flops 6712197120 | bytes 25231360 | tf_op jit(solution)/shard_map/dot_general | solution.py:23
  288.2 65.6 %all-gather.6.cloned.1.call-done = bf16[4096,2560]{1,0:T(8,128)(2,1)} async-done(((bf16[128,2560]{1,0:T(8,128)(2,1)}), bf16[4096,2560]{1,0:T(8,128)(2,1)}) %all-gather.6.cloned.1.call-update) | async-done | bytes 20971536 | tf_op jit(solution)/shard_map/all_gather | solution.py:30
  353.8 0.0 copy-done.6
  353.8 13.9 %fusion.6 = bf16[4096,320]{0,1:T(8,128)(2,1)S(1)} fusion(bf16[4096,320]{0,1:T(8,128)(2,1)} %convolution_convert_fusion.1, bf16[4096,2560]{1,0:T(8,128)(2,1)} %all-gather.6.cloned.1.call-done, bf16[320,2560]{1,0:T(8,128)(2,1)S(1)} %copy-done.6), kind=kOutput, calls=%fused_computation.17 | convolution fusion | flops 6741032960 | bytes 27852800 | tf_op jit(solution)/shard_map/dot_general | solution.py:31
  367.7 0.0 copy-start.4
  367.8 1.5 copy-done.4
  369.2 17.0 %fusion.30 = f32[4096,2560]{1,0:T(8,128)} fusion(bf16[4096,320]{0,1:T(8,128)(2,1)S(1)} %fusion.6, bf16[2560,320]{0,1:T(8,128)(2,1)S(1)} %copy-done), kind=kOutput, calls=%fused_computation.49 | convolution fusion | flops 6710886400 | bytes 46202880 | tf_op jit(solution)/shard_map/dot_general | solution.py:36
  386.2 0.1 reduce-scatter.8.cloned.1.call-update
  386.3 0.3 reduce-scatter.6.cloned.1.call-start
  386.6 21.5 %fusion.28 = f32[4096,2560]{1,0:T(8,128)} fusion(bf16[320,2560]{1,0:T(8,128)(2,1)S(1)} %copy-done.6, bf16[4096,320]{0,1:T(8,128)(2,1)} %convolution_convert_fusion.1), kind=kOutput, calls=%fused_computation.48 | convolution fusion | flops 6723993600 | bytes 46202880 | tf_op jit(solution)/shard_map/dot_general | solution.py:26
  408.0 0.0 copy-start.2
  408.0 0.0 copy-start.5
  408.0 0.1 reduce-scatter.6.cloned.1.call-update
  408.1 0.3 all-gather.8.cloned.1.call-start
  408.4 160.2 %reduce-scatter.8.cloned.1.call-done = f32[128,2560]{1,0:T(8,128)} async-done(((f32[4096,2560]{1,0:T(8,128)}), f32[128,2560]{1,0:T(8,128)}) %reduce-scatter.8.cloned.1.call-update) | async-done | bytes 1310736 | tf_op jit(solution)/shard_map/reduce_scatter | solution.py:37
  568.6 0.0 copy-done.2
  568.6 1.6 fusion.24
  570.2 185.2 %reduce-scatter.6.cloned.1.call-done = f32[128,2560]{1,0:T(8,128)} async-done(((f32[4096,2560]{1,0:T(8,128)}), f32[128,2560]{1,0:T(8,128)}) %reduce-scatter.6.cloned.1.call-update) | async-done | bytes 1310736 | tf_op jit(solution)/shard_map/reduce_scatter | solution.py:27
  755.4 0.0 copy-done.5
  755.4 3.3 fusion.21
  758.7 0.1 all-gather.8.cloned.1.call-update
  758.8 0.0 copy-start.3
  758.8 13.1 %fusion.31 = f32[2560,320]{0,1:T(8,128)} fusion(bf16[4096,320]{0,1:T(8,128)(2,1)} %copy-done.4, bf16[4096,2560]{1,0:T(8,128)(2,1)} %all-gather.4.cloned.1.call-done), kind=kOutput, calls=%fused_computation.50 | convolution fusion | flops 6710886400 | bytes 26869760 | tf_op jit(solution)/shard_map/dot_general | solution.py:35
  771.9 0.0 copy-done.3
  771.9 13.4 %fusion.26 = f32[320,2560]{1,0:T(8,128)} fusion(bf16[4096,2560]{1,0:T(8,128)(2,1)} %all-gather.6.cloned.1.call-done, bf16[4096,320]{0,1:T(8,128)(2,1)S(1)} %copy-done.3), kind=kOutput, calls=%fused_computation.47 | convolution fusion | flops 6723993600 | bytes 26869760 | tf_op jit(solution)/shard_map/dot_general | solution.py:32
  785.3 51.0 %all-gather.8.cloned.1.call-done = bf16[4096,2560]{1,0:T(8,128)(2,1)} async-done(((bf16[128,2560]{1,0:T(8,128)(2,1)}), bf16[4096,2560]{1,0:T(8,128)(2,1)}) %all-gather.8.cloned.1.call-update) | async-done | bytes 20971536 | tf_op jit(solution)/shard_map/all_gather | solution.py:41
  836.3 70.2 %scatter_custom_fusion = f32[1600,2560]{1,0:T(8,128)} fusion(s32[4096]{0:T(1024)} %get-tuple-element.6, bf16[4096,2560]{1,0:T(8,128)(2,1)} %all-gather.8.cloned.1.call-done, f32[]{:T(128)} %constant.21.clone.1), kind=kCustom, calls=%fused_computation.2 | custom fusion | flops 20971520 | bytes 37356032 | tf_op jit(solution)/shard_map/scatter-add | solution.py:43
  906.6 0.0 copy-done.1
  (4 shorter events, 0.0 us)
Async XLA Ops:
  7.2 268.0 %copy-start = (bf16[2560,320]{0,1:T(8,128)(2,1)S(1)}, bf16[2560,320]{0,1:T(8,128)(2,1)}, u32[]{:S(2)}) copy-start(bf16[2560,320]{0,1:T(8,128)(2,1)} %param.9) | copy-start | bytes 4915204
  7.2 186.3 %reduce-scatter.4.cloned.1.call-start = ((), (), s32[]{:S(2)}) async-start(), calls=%async_computation.3 | async-start | bytes 21626880 | tf_op jit(solution)/shard_map/reduce_scatter | solution.py:17
  70.1 0.7 copy-start.7
  70.1 205.0 %all-gather.4.cloned.1.call-start = ((), (), s32[]{:S(2)}) async-start(), calls=%async_computation.4 | async-start | bytes 21626880 | tf_op jit(solution)/shard_map/all_gather | solution.py:22
  197.0 156.8 %all-gather.6.cloned.1.call-start = ((), (), s32[]{:S(2)}) async-start(), calls=%async_computation.6 | async-start | bytes 21626880 | tf_op jit(solution)/shard_map/all_gather | solution.py:30
  197.8 156.0 %copy-start.6 = (bf16[320,2560]{1,0:T(8,128)(2,1)S(1)}, bf16[320,2560]{1,0:T(8,128)(2,1)}, u32[]{:S(2)}) copy-start(bf16[320,2560]{1,0:T(8,128)(2,1)} %param.10) | copy-start | bytes 4915204
  197.8 370.8 %reduce-scatter.8.cloned.1.call-start = ((), (), s32[]{:S(2)}) async-start(), calls=%async_computation.7 | async-start | bytes 43253760 | tf_op jit(solution)/shard_map/reduce_scatter | solution.py:37
  367.7 1.5 copy-start.4
  386.3 369.1 %reduce-scatter.6.cloned.1.call-start = ((), (), s32[]{:S(2)}) async-start(), calls=%async_computation.5 | async-start | bytes 43253760 | tf_op jit(solution)/shard_map/reduce_scatter | solution.py:27
  408.0 160.6 %copy-start.2 = (bf16[128,2560]{1,0:T(8,128)(2,1)S(1)}, bf16[128,2560]{1,0:T(8,128)(2,1)}, u32[]{:S(2)}) copy-start(bf16[128,2560]{1,0:T(8,128)(2,1)} %reduce-scatter.4.cloned.1.call-done) | copy-start | bytes 1966084
  408.0 347.4 %copy-start.5 = (bf16[128,2560]{1,0:T(8,128)(2,1)S(1)}, bf16[128,2560]{1,0:T(8,128)(2,1)}, u32[]{:S(2)}) copy-start(bf16[128,2560]{1,0:T(8,128)(2,1)} %param.11) | copy-start | bytes 1966084
  408.1 428.3 %all-gather.8.cloned.1.call-start = ((), (), s32[]{:S(2)}) async-start(), calls=%async_computation.8 | async-start | bytes 21626880 | tf_op jit(solution)/shard_map/all_gather | solution.py:41
  758.8 13.2 %copy-start.3 = (bf16[4096,320]{0,1:T(8,128)(2,1)S(1)}, bf16[4096,320]{0,1:T(8,128)(2,1)}, u32[]{:S(2)}) copy-start(bf16[4096,320]{0,1:T(8,128)(2,1)} %convolution_convert_fusion.1) | copy-start | bytes 7864324
  836.3 70.2 %copy-start.1 = (bf16[2560,320]{0,1:T(8,128)(2,1)S(1)}, bf16[2560,320]{0,1:T(8,128)(2,1)}, u32[]{:S(2)}) copy-start(bf16[2560,320]{0,1:T(8,128)(2,1)} %param.9) | copy-start | bytes 4915204
Sparse Core Ops, SparseCore 0:
  70.3 123.1 reduce-scatter.3
  197.1 78.0 all-gather.3
  277.3 76.4 all-gather.5
  386.4 182.1 reduce-scatter.7
  572.3 183.0 reduce-scatter.5
  758.9 77.3 all-gather.7
where the time goes:
time: 914 us; the launch traced here: 913 us
  waiting for transfers between devices  663 us (73%)
  other arithmetic  99.4 us (11%)
  matrix products  91.9 us (10%)
  local copies, waits for them, and re-layouts  44.1 us (5%)
  between operations  14.2 us (2%)
    reduce_scatter x1, waiting for transfers between devices, shard_step(): mlp_out = lax.psum_scatter(mlp_part, 'tp', scatter_dimension=0, tiled=True)  185 us
    reduce_scatter x1, waiting for transfers between devices, shard_step(): lax.psum_scatter(d_norm_part, 'tp', scatter_dimension=0, tiled=True)  160 us
    reduce_scatter x1, waiting for transfers between devices, shard_step(): lax.psum_scatter(lookup_part, 'tp', scatter_dimension=0, tiled=True)  123 us
    all_gather x1, waiting for transfers between devices, shard_step(): normed = lax.all_gather(normed_local, 'tp', axis=0, tiled=True)  77.1 us
    scatter-add x1, other arithmetic, shard_step(): jax.ops.segment_sum(d_emb_full.astype(jnp.float32), target_rows, num_segm...  70.2 us
    all_gather x1, waiting for transfers between devices, shard_step(): d_out_full = lax.all_gather(d_out, 'tp', axis=0, tiled=True)  65.6 us
    all_gather x1, waiting for transfers between devices, shard_step(): d_emb_full = lax.all_gather(d_emb, 'tp', axis=0, tiled=True)  51 us
    gather x1, local copies, waits for them, and re-layouts, shard_step(): table_rows = jnp.take(emb_table, jnp.where(is_owned, local_ids, 0), axis=0)  42 us
  transfers between devices with their start and end apart: 6, of which 6 were waited for; matrix products, arithmetic and copies ran while one was open for 7% of the time, Pallas kernels for 0%

commit v1 on v0

v1 whole, which is shorter than its diff:
```python
import jax
import jax.numpy as jnp
from jax import lax
from jax.sharding import PartitionSpec as P

EPS = 1e-6
CHUNKS = 2


def solution(mesh):
    n_dev = mesh.shape["tp"]
    planes = [list(range(c, n_dev, 2)) for c in range(2)]
    swap = [(i, i ^ 1) for i in range(n_dev)]
    f32, bf16 = jnp.float32, jnp.bfloat16

    def gather_plane(v):
        return lax.all_gather(v, "tp", axis=0, tiled=True, axis_index_groups=planes)

    def scatter_plane(v):
        return lax.psum_scatter(v, "tp", scatter_dimension=0, tiled=True, axis_index_groups=planes)

    def dot(a, b, ca, cb):
        return lax.dot_general(a, b, (((ca,), (cb,)), ((), ())), preferred_element_type=f32)

    def shard_step(token_ids, emb_table, norm_gain, w_in, w_out, d_out):
        rank = lax.axis_index("tp")
        core = rank % 2
        rows = d_out.shape[0]
        width = w_in.shape[1]
        vocab = emb_table.shape[0]
        part = rows // CHUNKS
        own_base = rank * vocab
        sib_base = (rank + 1 - 2 * core) * vocab
        ids_blocks = token_ids.reshape(n_dev // 2, 2, rows)
        ids_plane = lax.dynamic_index_in_dim(ids_blocks, core, axis=1, keepdims=False).reshape(-1, 1)
        vocab_col = lax.broadcasted_iota(jnp.int32, (1, vocab), 1)
        vocab_row = lax.broadcasted_iota(jnp.int32, (vocab, 1), 0)
        gain_f32 = norm_gain.astype(f32)

        table_sib = lax.ppermute(emb_table, "tp", swap)
        w_out2 = jnp.concatenate([w_out, lax.ppermute(w_out, "tp", swap)], axis=0)
        w_in2 = jnp.concatenate([w_in, lax.ppermute(w_in, "tp", swap)], axis=1)

        d_full = gather_plane(d_out)

        own = (ids_plane - own_base == vocab_col).astype(bf16)
        sib = (ids_plane - sib_base == vocab_col).astype(bf16)
        look = (dot(own, emb_table, 1, 0) + dot(sib, table_sib, 1, 0)).astype(bf16)
        look, d_full = lax.optimization_barrier((look, d_full))
        emb = scatter_plane(look).astype(f32)
        inv = lax.rsqrt(jnp.mean(emb * emb, axis=-1, keepdims=True) + EPS)
        normed_local = (emb * inv * gain_f32).astype(bf16)
        normed = [gather_plane(normed_local[k * part:(k + 1) * part]) for k in range(CHUNKS)]

        d_hidden = dot(d_full, w_out2, 1, 1).astype(bf16)
        d_hidden_c = d_hidden.reshape(n_dev // 2, CHUNKS, part, 2 * width)
        hidden, d_pre, d_normed = [], [], []
        for k in range(CHUNKS):
            pre_act = dot(normed[k], w_in2, 1, 0).astype(bf16)
            act_f32, gelu_vjp = jax.vjp(jax.nn.gelu, pre_act.astype(f32))
            hidden.append(act_f32.astype(bf16).reshape(n_dev // 2, 1, part, 2 * width))
            (d_pre_f32,) = gelu_vjp(d_hidden_c[:, k].reshape(-1, 2 * width).astype(f32))
            d_pre.append(d_pre_f32.astype(bf16))
            d_normed.append(scatter_plane(dot(d_pre[k], w_in2, 1, 1)))
        hidden = jnp.concatenate(hidden, axis=1).reshape(-1, 2 * width)
        y_part = dot(hidden, w_out2, 1, 0)

        d_w_in2 = sum(dot(normed[k], d_pre[k], 0, 0) for k in range(CHUNKS))
        d_w_out2 = dot(hidden, d_full, 0, 0)
        d_w_in = d_w_in2[:, :width] + lax.ppermute(d_w_in2[:, width:], "tp", swap)
        d_w_out = d_w_out2[:width] + lax.ppermute(d_w_out2[width:], "tp", swap)

        d_scaled = jnp.concatenate(d_normed, axis=0) * gain_f32
        row_proj = jnp.mean(d_scaled * emb, axis=-1, keepdims=True)
        d_emb = (d_out.astype(f32) + inv * (d_scaled - emb * inv * inv * row_proj)).astype(bf16)
        d_emb_full = lax.all_gather(d_emb, "tp", axis=0, tiled=True)
        y_part, d_emb_full = lax.optimization_barrier((y_part, d_emb_full))
        block_out = (emb + scatter_plane(y_part)).astype(bf16)

        hit = (token_ids.reshape(1, -1) - own_base == vocab_row).astype(bf16)
        d_table = dot(hit, d_emb_full, 1, 0)
        return block_out, d_table, d_w_in, d_w_out

    return jax.shard_map(
        shard_step,
        mesh=mesh,
        in_specs=(P("dp"), P("tp", None), P(None), P(None, "tp"), P("tp", None), P(("dp", "tp"), None)),
        out_specs=(P(("dp", "tp"), None), P(("dp", "tp"), None), P("dp", "tp"), P(("dp", "tp"), None)),
        check_vma=False,
    )
```

time: 914 us -> 686 us (0.75)
  waiting for transfers between devices: 663 us -> 478 us
  other arithmetic: 99.4 us -> 16.2 us
  matrix products: 91.9 us -> 159 us
  local copies, waits for them, and re-layouts: 44.1 us -> 3.84 us
    reduce_scatter x3 -> x4, waiting for transfers between devices: 468 us -> 305 us  [scatter_plane(): lax.psum_scatter(v, 'tp', scatter_dimension=0, tiled=True, axis_index_gro...]
    scatter-add x1 -> x0, other arithmetic: 70.2 us -> none  [shard_step(): jax.ops.segment_sum(d_emb_full.astype(jnp.float32), target_rows, num_segm...]
    dot_general x6 -> x12, matrix products: 91.9 us -> 159 us  [dot(): lax.dot_general(a, b, (((ca,), (cb,)), ((), ())), preferred_element_type=...]
    all_gather x2 -> x3, waiting for transfers between devices: 143 us -> 99.3 us  [gather_plane(): return lax.all_gather(v, 'tp', axis=0, tiled=True, axis_index_groups=planes)]
    gather x1 -> x0, local copies, waits for them, and re-layouts: 42 us -> none  [shard_step(): table_rows = jnp.take(emb_table, jnp.where(is_owned, local_ids, 0), axis=0)]
    select_n x2 -> x0, other arithmetic: 19.9 us -> none  [the longest x1 18.6 us: shard_step(): jnp.where(is_owned[:, None], table_rows, jnp.zeros((), table_rows.dtype))]
    all_gather x1, waiting for transfers between devices: 51 us -> 63.6 us  [shard_step(): d_emb_full = lax.all_gather(d_emb, 'tp', axis=0, tiled=True)]
  transfers between devices with their start and end apart: 6 -> 13, of which waited for: 6 -> 11; matrix products, arithmetic and copies ran while one was open for 7% -> 25% of each run, Pallas kernels for 0% -> 0%
where the time goes in v1:
time: 686 us; the launch traced here: 679 us
  waiting for transfers between devices  478 us (70%)
  matrix products  159 us (23%)
  other arithmetic  16.2 us (2%)
  between operations  14.9 us (2%)
    reduce_scatter x4, waiting for transfers between devices, scatter_plane(): lax.psum_scatter(v, 'tp', scatter_dimension=0, tiled=True, axis_index_gro...  305 us
    dot_general x12, matrix products, dot(): lax.dot_general(a, b, (((ca,), (cb,)), ((), ())), preferred_element_type=...  159 us
    all_gather x3, waiting for transfers between devices, gather_plane(): return lax.all_gather(v, 'tp', axis=0, tiled=True, axis_index_groups=planes)  99.3 us
    all_gather x1, waiting for transfers between devices, shard_step(): d_emb_full = lax.all_gather(d_emb, 'tp', axis=0, tiled=True)  63.6 us
  transfers between devices with their start and end apart: 13, of which 11 were waited for; matrix products, arithmetic and copies ran while one was open for 25% of the time, Pallas kernels for 0%

profile of v1, /device:TPU:97, one launch (start us, length us, event | category | flops | bytes accessed | tf_op | source)
XLA Modules:
  0.0 678.9 jit_solution(12847310368350639919)
XLA Ops:
  7.2 0.7 all-gather.5.cloned.1.call-update
  8.0 2.1 collective-permute-start
  10.2 0.7 broadcast_subtract_fusion.1
  10.9 21.8 %fusion.1 = f32[2048,2560]{1,0:T(8,128)S(1)} fusion(bf16[1600,2560]{1,0:T(8,128)(2,1)} %param.7, s32[2048]{0:T(1024)S(1)} %bitcast.49), kind=kOutput, calls=%fused_computation.5 | convolution fusion | flops 16780492800 | bytes 29171712 | tf_op jit(solution)/shard_map/dot_general | solution.py:23
  32.7 24.5 %add_convert_fusion = bf16[2048,2560]{1,0:T(8,128)(2,1)} fusion(f32[2048,2560]{1,0:T(8,128)S(1)} %fusion.1, bf16[1600,2560]{1,0:T(8,128)(2,1)} %collective-permute-done, s32[2048]{0:T(1024)S(1)} %bitcast.48), kind=kOutput, calls=%fused_computation.2 | convolution fusion | flops 16790978560 | bytes 39657472 | tf_op jit(solution)/shard_map/dot_general | solution.py:23
  57.3 31.5 %all-gather.5.cloned.1.call-done = bf16[2048,2560]{1,0:T(8,128)(2,1)} async-done(((bf16[128,2560]{1,0:T(8,128)(2,1)}), bf16[2048,2560]{1,0:T(8,128)(2,1)}) %all-gather.5.cloned.1.call-update) | async-done | bytes 10485776 | tf_op jit(solution)/shard_map/all_gather | solution.py:17
  89.0 87.4 %reduce-scatter.5.cloned.1.call-done = bf16[128,2560]{1,0:T(8,128)(2,1)} async-done(((bf16[2048,2560]{1,0:T(8,128)(2,1)}), bf16[128,2560]{1,0:T(8,128)(2,1)}) %reduce-scatter.5.cloned.1.call-update) | async-done | bytes 655376 | tf_op jit(solution)/shard_map/reduce_scatter | solution.py:20
  176.4 1.3 fusion.36
  177.7 1.3 fusion.30
  179.0 0.9 fusion.40
  180.0 0.6 all-gather.9.cloned.1.call-update
  180.6 0.6 reduce-scatter.7.cloned.1.call-start
  181.2 2.0 collective-permute-start.1
  183.2 0.1 collective-permute-start.2
  183.6 2.8 collective-permute-done.1
  186.5 2.2 collective-permute-done.2
  188.8 8.5 %convolution_convert_fusion = bf16[2048,640]{1,0:T(8,128)(2,1)S(1)} fusion(bf16[2048,2560]{1,0:T(8,128)(2,1)S(1)} %copy-done.11, bf16[640,2560]{1,0:T(8,128)(2,1)S(1)} %constant_dynamic-update-slice_fusion.2), kind=kOutput, calls=%fused_computation.27 | convolution fusion | flops 6712197120 | bytes 16384000 | tf_op jit(solution)/shard_map/dot_general | solution.py:23
  197.4 0.2 fusion.39
  197.6 33.5 %all-gather.7.cloned.1.call-done = bf16[1024,2560]{1,0:T(8,128)(2,1)} async-done(((bf16[64,2560]{1,0:T(8,128)(2,1)}), bf16[1024,2560]{1,0:T(8,128)(2,1)}) %all-gather.7.cloned.1.call-update) | async-done | bytes 5242896 | tf_op jit(solution)/shard_map/all_gather | solution.py:17
  231.2 10.4 %fusion.10 = (bf16[1024,640]{1,0:T(8,128)(2,1)S(1)}, bf16[1024,640]{1,0:T(8,128)(2,1)}) fusion(bf16[16,1,64,640]{3,2,1,0:T(8,128)(2,1)S(1)} %get-tuple-element.12, bf16[1024,2560]{1,0:T(8,128)(2,1)} %all-gather.7.cloned.1.call-done, bf16[2560,640]{0,1:T(8,128)(2,1)} %copy-done.6), kind=kOutput, calls=%fused_computation.30 | convolution fusion | flops 3371827200 | bytes 12451840 | tf_op jit(solution)/shard_map/dot_general | solution.py:23
  241.6 1.1 copy-done.12
  242.7 6.8 fusion.42
  249.5 0.2 reduce-scatter.9.cloned.1.call-start
  249.8 34.2 %all-gather.9.cloned.1.call-done = bf16[1024,2560]{1,0:T(8,128)(2,1)} async-done(((bf16[64,2560]{1,0:T(8,128)(2,1)}), bf16[1024,2560]{1,0:T(8,128)(2,1)}) %all-gather.9.cloned.1.call-update) | async-done | bytes 5242896 | tf_op jit(solution)/shard_map/all_gather | solution.py:17
  284.0 10.4 %fusion.13 = (bf16[1024,640]{1,0:T(8,128)(2,1)S(1)}, bf16[1024,640]{1,0:T(8,128)(2,1)}) fusion(bf16[16,1,64,640]{3,2,1,0:T(8,128)(2,1)S(1)} %get-tuple-element.13, bf16[1024,2560]{1,0:T(8,128)(2,1)} %all-gather.9.cloned.1.call-done, bf16[2560,640]{0,1:T(8,128)(2,1)} %copy-done.6), kind=kOutput, calls=%fused_computation.33 | convolution fusion | flops 3371827200 | bytes 12451840 | tf_op jit(solution)/shard_map/dot_general | solution.py:23
  294.4 6.8 %fusion.43 = f32[1024,2560]{1,0:T(8,128)} fusion(bf16[1024,640]{1,0:T(8,128)(2,1)S(1)} %get-tuple-element.16, bf16[2560,640]{0,1:T(8,128)(2,1)S(1)} %copy-done.8), kind=kOutput, calls=%fused_computation.80 | convolution fusion | flops 3355443200 | bytes 15073280 | tf_op jit(solution)/shard_map/dot_general | solution.py:23
  301.3 69.5 %reduce-scatter.7.cloned.1.call-done = f32[64,2560]{1,0:T(8,128)} async-done(((f32[1024,2560]{1,0:T(8,128)}), f32[64,2560]{1,0:T(8,128)}) %reduce-scatter.7.cloned.1.call-update) | async-done | bytes 655376 | tf_op jit(solution)/shard_map/reduce_scatter | solution.py:20
  370.8 87.4 %reduce-scatter.9.cloned.1.call-done = f32[64,2560]{1,0:T(8,128)} async-done(((f32[1024,2560]{1,0:T(8,128)}), f32[64,2560]{1,0:T(8,128)}) %reduce-scatter.9.cloned.1.call-update) | async-done | bytes 655376 | tf_op jit(solution)/shard_map/reduce_scatter | solution.py:20
  458.3 1.5 fusion.37
  459.8 2.6 fusion.35
  462.5 0.3 reduce-scatter.11.cloned.1.call-start
  462.8 2.1 pad_maximum_fusion
  464.9 0.6 copy-done.5
  465.5 11.5 %fusion.41 = f32[2048,2560]{1,0:T(8,128)} fusion(bf16[2048,640]{1,0:T(8,128)(2,1)S(1)} %bitcast.42, bf16[640,2560]{1,0:T(8,128)(2,1)S(1)} %copy-done.5), kind=kOutput, calls=%fused_computation.78 | convolution fusion | flops 6710886400 | bytes 26869760 | tf_op jit(solution)/shard_map/dot_general | solution.py:23
  477.0 63.6 %all-gather.11.cloned.1.call-done = bf16[4096,2560]{1,0:T(8,128)(2,1)} async-done(((bf16[128,2560]{1,0:T(8,128)(2,1)}), bf16[4096,2560]{1,0:T(8,128)(2,1)}) %all-gather.11.cloned.1.call-update) | async-done | bytes 20971536 | tf_op jit(solution)/shard_map/all_gather | solution.py:76
  540.8 6.2 fusion.44
  547.0 6.2 convolution_add_fusion
  553.2 0.2 slice.37
  553.4 0.4 collective-permute-start.3
  553.8 7.0 %fusion.45 = f32[640,2560]{1,0:T(8,128)S(1)} fusion(bf16[2048,640]{1,0:T(8,128)(2,1)S(1)} %bitcast.43, bf16[2048,2560]{1,0:T(8,128)(2,1)S(1)} %bitcast.51), kind=kOutput, calls=%fused_computation.82 | convolution fusion | flops 6710886400 | bytes 19660800 | tf_op jit(solution)/shard_map/dot_general | solution.py:23
  560.8 0.2 slice.39
  561.1 0.3 collective-permute-start.4
  561.5 2.2 slice_add_fusion.1
  563.7 3.3 collective-permute-done.4
  567.0 2.2 slice_add_fusion
  569.2 39.1 %fusion = f32[1600,2560]{1,0:T(8,128)} fusion(bf16[4096,2560]{1,0:T(8,128)(2,1)} %all-gather.11.cloned.1.call-done, s32[4096]{0:T(1024)S(1)} %broadcast_subtract_fusion), kind=kOutput, calls=%fused_computation.1 | convolution fusion | flops 33560985600 | bytes 37371904 | tf_op jit(solution)/shard_map/dot_general | solution.py:23
  608.2 61.1 %reduce-scatter.11.cloned.1.call-done = f32[128,2560]{1,0:T(8,128)} async-done(((f32[2048,2560]{1,0:T(8,128)}), f32[128,2560]{1,0:T(8,128)}) %reduce-scatter.11.cloned.1.call-update) | async-done | bytes 1310736 | tf_op jit(solution)/shard_map/reduce_scatter | solution.py:20
  669.3 2.3 fusion.38
  (56 shorter events, 1.3 us)
Async XLA Ops:
  7.2 81.6 %all-gather.5.cloned.1.call-start = ((), (), s32[]{:S(2)}) async-start(), calls=%async_computation.4 | async-start | bytes 11141120 | tf_op jit(solution)/shard_map/all_gather | solution.py:17
  8.0 168.4 %reduce-scatter.5.cloned.1.call-start = ((), (), s32[]{:S(2)}) async-start(), calls=%async_computation.5 | async-start | bytes 11141120 | tf_op jit(solution)/shard_map/reduce_scatter | solution.py:20
  8.0 24.7 %collective-permute-start = (bf16[1600,2560]{1,0:T(8,128)(2,1)}, bf16[1600,2560]{1,0:T(8,128)(2,1)}, u32[]{:S(2)}, u32[]{:S(2)}) collective-permute-start(bf16[1600,2560]{1,0:T(8,128)(2,1)} %param.7), channel_id=1, source_target_pairs={{0,1},{1,0},{2,3},{3,2},{4,5},{5,4},{6,7},{7,6},{8,9},{9,8},{10,11... | collective-permute-start | bytes 24576008 | tf_op jit(solution)/shard_map/ppermute | solution.py:40
  57.3 31.7 %copy-start.10 = (bf16[2560]{0:T(1024)(128)(2,1)S(1)}, bf16[2560]{0:T(1024)(128)(2,1)}, u32[]{:S(2)}) copy-start(bf16[2560]{0:T(1024)(128)(2,1)} %param.8) | copy-start | bytes 15364
  88.9 92.3 %copy-start.2 = (bf16[2560,320]{0,1:T(8,128)(2,1)S(1)}, bf16[2560,320]{0,1:T(8,128)(2,1)}, u32[]{:S(2)}) copy-start(bf16[2560,320]{0,1:T(8,128)(2,1)} %param.9) | copy-start | bytes 4915204
  88.9 94.3 %copy-start.3 = (bf16[320,2560]{1,0:T(8,128)(2,1)S(1)}, bf16[320,2560]{1,0:T(8,128)(2,1)}, u32[]{:S(2)}) copy-start(bf16[320,2560]{1,0:T(8,128)(2,1)} %param.10) | copy-start | bytes 4915204
  88.9 142.3 %all-gather.7.cloned.1.call-start = ((), (), s32[]{:S(2)}) async-start(), calls=%async_computation.6 | async-start | bytes 5570560 | tf_op jit(solution)/shard_map/all_gather | solution.py:17
  180.0 104.0 %all-gather.9.cloned.1.call-start = ((), (), s32[]{:S(2)}) async-start(), calls=%async_computation.7 | async-start | bytes 5570560 | tf_op jit(solution)/shard_map/all_gather | solution.py:17
  180.6 190.2 %reduce-scatter.7.cloned.1.call-start = ((), (), s32[]{:S(2)}) async-start(), calls=%async_computation.8 | async-start | bytes 11141120 | tf_op jit(solution)/shard_map/reduce_scatter | solution.py:20
  181.2 5.1 collective-permute-start.1
  183.2 5.5 collective-permute-start.2
  183.4 5.5 copy-start.11
  186.5 2.2 copy-start.6
  188.8 8.6 %copy-start.4 = (bf16[640,2560]{1,0:T(8,128)(2,1)}, bf16[640,2560]{1,0:T(8,128)(2,1)S(1)}, u32[]{:S(2)}) copy-start(bf16[640,2560]{1,0:T(8,128)(2,1)S(1)} %constant_dynamic-update-slice_fusion.2) | copy-start | bytes 9830404
  231.2 11.5 %copy-start.7 = (bf16[2560,640]{0,1:T(8,128)(2,1)S(1)}, bf16[2560,640]{0,1:T(8,128)(2,1)}, u32[]{:S(2)}) copy-start(bf16[2560,640]{0,1:T(8,128)(2,1)} %copy-done.6) | copy-start | bytes 9830404
  241.6 1.1 copy-start.12
  249.5 208.7 %reduce-scatter.9.cloned.1.call-start = ((), (), s32[]{:S(2)}) async-start(), calls=%async_computation.9 | async-start | bytes 11141120 | tf_op jit(solution)/shard_map/reduce_scatter | solution.py:20
  284.0 10.4 %copy-start.8 = (bf16[2560,640]{0,1:T(8,128)(2,1)S(1)}, bf16[2560,640]{0,1:T(8,128)(2,1)}, u32[]{:S(2)}) copy-start(bf16[2560,640]{0,1:T(8,128)(2,1)} %copy-done.6) | copy-start | bytes 9830404
  294.4 6.8 %copy-start.13 = (bf16[1024,640]{1,0:T(8,128)(2,1)}, bf16[1024,640]{1,0:T(8,128)(2,1)S(1)}, u32[]{:S(2)}) copy-start(bf16[1024,640]{1,0:T(8,128)(2,1)S(1)} %get-tuple-element.16) | copy-start | bytes 3932164
  301.2 157.1 %copy-start = (bf16[128,2560]{1,0:T(8,128)(2,1)S(1)}, bf16[128,2560]{1,0:T(8,128)(2,1)}, u32[]{:S(2)}) copy-start(bf16[128,2560]{1,0:T(8,128)(2,1)} %reduce-scatter.5.cloned.1.call-done) | copy-start | bytes 1966084
  301.2 158.6 %copy-start.1 = (bf16[128,2560]{1,0:T(8,128)(2,1)S(1)}, bf16[128,2560]{1,0:T(8,128)(2,1)}, u32[]{:S(2)}) copy-start(bf16[128,2560]{1,0:T(8,128)(2,1)} %param.11) | copy-start | bytes 1966084
  301.3 239.4 %all-gather.11.cloned.1.call-start = ((), (), s32[]{:S(2)}) async-start(), calls=%async_computation.10 | async-start | bytes 21626880 | tf_op jit(solution)/shard_map/all_gather | solution.py:76
  462.5 206.9 %reduce-scatter.11.cloned.1.call-start = ((), (), s32[]{:S(2)}) async-start(), calls=%async_computation.11 | async-start | bytes 22282240 | tf_op jit(solution)/shard_map/reduce_scatter | solution.py:20
  462.7 2.7 copy-start.5
  540.7 6.2 copy-start.14
  540.7 13.0 %slice-start = ((s8[10485760]{0:T(1024)(128)(4,1)}), s8[4194304]{0:T(1024)(128)(4,1)S(1)}, s32[]{:S(2)}) async-start(s8[10485760]{0:T(1024)(128)(4,1)} %bitcast.50), calls=%async_computation.12 | async-start | bytes 8388608
  540.7 13.0 %slice-start.1 = ((s8[10485760]{0:T(1024)(128)(4,1)}), s8[4194304]{0:T(1024)(128)(4,1)S(1)}, s32[]{:S(2)}) async-start(s8[10485760]{0:T(1024)(128)(4,1)} %bitcast.50), calls=%async_computation.13 | async-start | bytes 8388608
  547.0 6.8 %slice-start.2 = ((s8[10485760]{0:T(1024)(128)(4,1)}), s8[2097152]{0:T(1024)(128)(4,1)S(1)}, s32[]{:S(2)}) async-start(s8[10485760]{0:T(1024)(128)(4,1)} %bitcast.50), calls=%async_computation.14 | async-start | bytes 4194304
  553.4 8.1 %collective-permute-start.3 = (f32[2560,320]{0,1:T(8,128)S(1)}, f32[2560,320]{0,1:T(8,128)S(1)}, u32[]{:S(2)}, u32[]{:S(2)}) collective-permute-start(f32[2560,320]{0,1:T(8,128)S(1)} %slice.37), channel_id=1, source_target_pairs={{0,1},{1,0},{2,3},{3,2},{4,5},{5,4},{6,7},{7,6},{8,9},{9,8},{10,11... | collective-permute-start | bytes 9830408 | tf_op jit(solution)/shard_map/ppermute | solution.py:70
  560.8 0.7 copy-start.9
  561.1 5.9 collective-permute-start.4
Sparse Core Ops, SparseCore 0:
  10.0 78.7 all-gather.4
  92.6 83.7 reduce-scatter.4
  180.1 51.0 all-gather.6
  233.6 50.3 all-gather.8
  287.1 83.6 reduce-scatter.6
  374.5 83.6 reduce-scatter.8
  462.6 78.0 all-gather.10
  543.9 125.3 reduce-scatter.10

commit v2 on v1

--- a/solution.py
+++ b/solution.py
@@ -1,15 +1,185 @@
+import functools
+import math
+
 import jax
 import jax.numpy as jnp
 from jax import lax
+from jax.experimental import pallas as pl
+from jax.experimental.pallas import tpu as pltpu
 from jax.sharding import PartitionSpec as P
 
 EPS = 1e-6
-CHUNKS = 2
+STREAMS = 4
+
+
+def exchange_kernel(side, gain_ref, look_ref, x_ref, n_ref, ring1, ring2, s1, r1, s2, r2, t1, u1, t2, u2):
+    rows, dim = x_ref.shape
+    cols = dim // STREAMS
+    rank = lax.axis_index("tp")
+    core = lax.rem(rank, 2)
+    chip = rank // 2
+    y, x = chip // side, lax.rem(chip, side)
+    last = side - 1
+
+    def wrap(v):
+        return lax.rem(v + 2 * side, side)
+
+    def device(yy, xx):
+        return {"tp": (wrap(yy) * side + wrap(xx)) * 2 + core}
+
+    def sign(k):
+        return 1 if k % 2 == 0 else -1
+
+    def first(k):
+        return x if k < 2 else y
+
+    def second(k):
+        return y if k < 2 else x
+
+    def piece(ref, k, a, b):
+        block = (wrap(b) * side + wrap(a)) if k < 2 else (wrap(a) * side + wrap(b))
+        return ref.at[pl.ds(pl.multiple_of(block * rows, rows), rows), pl.ds(k * cols, cols)]
+
+    def next_first(k):
+        return device(y, x + sign(k)) if k < 2 else device(y + sign(k), x)
+
+    def next_second(k):
+        return device(y + sign(k), x) if k < 2 else device(y, x + sign(k))
+
+    def copy(src, dst, send, recv, to):
+        return pltpu.make_async_remote_copy(
+            src_ref=src, dst_ref=dst, send_sem=send, recv_sem=recv, device_id=to, device_id_type=pl.DeviceIdType.MESH
+        )
+
+    barrier = pltpu.get_barrier_semaphore()
+    for dy, dx in ((0, 1), (0, -1), (1, 0), (-1, 0)):
+        pl.semaphore_signal(barrier, inc=1, device_id=device(y + dy, x + dx), device_id_type=pl.DeviceIdType.MESH)
+    pl.semaphore_wait(barrier, 4)
+
+    every = range(STREAMS)
+    sent = []
+
+    def scatter_first(k, s, j, src):
+        return copy(src, ring1.at[k, s, j], s1.at[k, s, j], r1.at[k, s, j], next_first(k))
+
+    def scatter_second(k, m, src):
+        return copy(src, ring2.at[k, m], s2.at[k, m], r2.at[k, m], next_second(k))
+
+    def go(c):
+        c.start()
+        sent.append(c)
+
+    for j in range(side):
+        for k in every:
+            go(scatter_first(k, 0, j, piece(look_ref, k, first(k) - sign(k), second(k) - sign(k) * (1 + j))))
+    for s in range(last):
+        for j in range(side):
+            for k in every:
+                held = ring1.at[k, s, j]
+                scatter_first(k, s, j, held).wait_recv()
+                own = piece(look_ref, k, first(k) - sign(k) * (2 + s), second(k) - sign(k) * (1 + j))
+                held[...] += own[...]
+            for k in every:
+                held = ring1.at[k, s, j]
+                if s < last - 1:
+                    go(scatter_first(k, s + 1, j, held))
+                elif j == 0:
+                    go(scatter_second(k, 0, held))
+    for j in range(1, side):
+        for k in every:
+            held = ring2.at[k, j - 1]
+            scatter_second(k, j - 1, held).wait_recv()
+            total = held[...] + ring1[k, last - 1, j]
+            if j < last:
+                held[...] = total
+            else:
+                x_ref[:, pl.ds(k * cols, cols)] = total
+        if j < last:
+            for k in every:
+                go(scatter_second(k, j, ring2.at[k, j - 1]))
+
+    mine = pl.multiple_of(chip * rows, rows)
+    strip = 16
+
+    @pl.loop(0, rows // strip)
+    def _(i):
+        at = pl.ds(pl.multiple_of(i * strip, strip), strip)
+        e = x_ref[at, :].astype(jnp.float32)
+        r = lax.rsqrt(jnp.mean(e * e, axis=-1, keepdims=True) + EPS)
+        n_ref[pl.ds(pl.multiple_of(mine + i * strip, strip), strip), :] = (
+            e * r * gain_ref[...].astype(jnp.float32)
+        ).astype(jnp.bfloat16)
+
+    def gather_first(k, s):
+        p = piece(n_ref, k, first(k) - sign(k) * s, second(k))
+        return copy(p, p, t1.at[k, s], u1.at[k, s], next_first(k))
+
+    def gather_second(k, m, i):
+        p = piece(n_ref, k, first(k) - sign(k) * i, second(k) - sign(k) * m)
+        return copy(p, p, t2.at[k, m, i], u2.at[k, m, i], next_second(k))
+
+    def arrived_first(k, s):
+        p = piece(n_ref, k, first(k) - sign(k) * (s + 1), second(k))
+        copy(p, p, t1.at[k, s], u1.at[k, s], next_first(k)).wait_recv()
+
+    def arrived_second(k, m, i):
+        p = piece(n_ref, k, first(k) - sign(k) * i, second(k) - sign(k) * (m + 1))
+        copy(p, p, t2.at[k, m, i], u2.at[k, m, i], next_second(k)).wait_recv()
+        if m < last - 1:
+            go(gather_second(k, m + 1, i))
+
+    for k in every:
+        go(gather_first(k, 0))
+        go(gather_second(k, 0, 0))
+    for s in range(last):
+        for k in every:
+            arrived_first(k, s)
+            if s < last - 1:
+                go(gather_first(k, s + 1))
+            go(gather_second(k, 0, s + 1))
+        for k in every:
+            arrived_second(k, 0, s)
+    for m in range(last):
+        for i in range(last if m == 0 else 0, side):
+            for k in every:
+                arrived_second(k, m, i)
+    for c in sent:
+        c.wait_send()
+
+
+def exchange(look, gain, rows, side):
+    total, dim = look.shape
+    cols = dim // STREAMS
+    last = side - 1
+    dma = pltpu.SemaphoreType.DMA
+    vmem = pl.BlockSpec(memory_space=pltpu.VMEM)
+    return pl.pallas_call(
+        functools.partial(exchange_kernel, side),
+        out_shape=(jax.ShapeDtypeStruct((rows, dim), look.dtype), jax.ShapeDtypeStruct((total, dim), look.dtype)),
+        in_specs=[vmem, vmem],
+        out_specs=(vmem, vmem),
+        scratch_shapes=[
+            pltpu.VMEM((STREAMS, last, side, rows, cols), look.dtype),
+            pltpu.VMEM((STREAMS, last, rows, cols), look.dtype),
+            dma((STREAMS, last, side)),
+            dma((STREAMS, last, side)),
+            dma((STREAMS, last)),
+            dma((STREAMS, last)),
+            dma((STREAMS, last)),
+            dma((STREAMS, last)),
+            dma((STREAMS, last, side)),
+            dma((STREAMS, last, side)),
+        ],
+        compiler_params=pltpu.CompilerParams(collective_id=0, has_side_effects=True),
+        cost_estimate=pl.CostEstimate(flops=100_000_000_000, bytes_accessed=4 * total * dim, transcendentals=0),
+        name="exchange",
+    )(gain.reshape(1, dim), look)
 
 
 def solution(mesh):
     n_dev = mesh.shape["tp"]
     planes = [list(range(c, n_dev, 2)) for c in range(2)]
+    side = math.isqrt(n_dev // 2)
     swap = [(i, i ^ 1) for i in range(n_dev)]
     f32, bf16 = jnp.float32, jnp.bfloat16
 
@@ -28,7 +198,6 @@
         rows = d_out.shape[0]
         width = w_in.shape[1]
         vocab = emb_table.shape[0]
-        part = rows // CHUNKS
         own_base = rank * vocab
         sib_base = (rank + 1 - 2 * core) * vocab
         ids_blocks = token_ids.reshape(n_dev // 2, 2, rows)
@@ -46,31 +215,25 @@
         own = (ids_plane - own_base == vocab_col).astype(bf16)
         sib = (ids_plane - sib_base == vocab_col).astype(bf16)
         look = (dot(own, emb_table, 1, 0) + dot(sib, table_sib, 1, 0)).astype(bf16)
-        look, d_full = lax.optimization_barrier((look, d_full))
-        emb = scatter_plane(look).astype(f32)
+        emb, normed = exchange(look, norm_gain, rows, side)
+        emb = emb.astype(f32)
         inv = lax.rsqrt(jnp.mean(emb * emb, axis=-1, keepdims=True) + EPS)
-        normed_local = (emb * inv * gain_f32).astype(bf16)
-        normed = [gather_plane(normed_local[k * part:(k + 1) * part]) for k in range(CHUNKS)]
 
         d_hidden = dot(d_full, w_out2, 1, 1).astype(bf16)
-        d_hidden_c = d_hidden.reshape(n_dev // 2, CHUNKS, part, 2 * width)
-        hidden, d_pre, d_normed = [], [], []
-        for k in range(CHUNKS):
-            pre_act = dot(normed[k], w_in2, 1, 0).astype(bf16)
-            act_f32, gelu_vjp = jax.vjp(jax.nn.gelu, pre_act.astype(f32))
-            hidden.append(act_f32.astype(bf16).reshape(n_dev // 2, 1, part, 2 * width))
-            (d_pre_f32,) = gelu_vjp(d_hidden_c[:, k].reshape(-1, 2 * width).astype(f32))
-            d_pre.append(d_pre_f32.astype(bf16))
-            d_normed.append(scatter_plane(dot(d_pre[k], w_in2, 1, 1)))
-        hidden = jnp.concatenate(hidden, axis=1).reshape(-1, 2 * width)
+        pre_act = dot(normed, w_in2, 1, 0).astype(bf16)
+        act_f32, gelu_vjp = jax.vjp(jax.nn.gelu, pre_act.astype(f32))
+        hidden = act_f32.astype(bf16)
+        (d_pre_f32,) = gelu_vjp(d_hidden.astype(f32))
+        d_pre = d_pre_f32.astype(bf16)
+        d_normed = scatter_plane(dot(d_pre, w_in2, 1, 1))
         y_part = dot(hidden, w_out2, 1, 0)
 
-        d_w_in2 = sum(dot(normed[k], d_pre[k], 0, 0) for k in range(CHUNKS))
+        d_w_in2 = dot(normed, d_pre, 0, 0)
         d_w_out2 = dot(hidden, d_full, 0, 0)
         d_w_in = d_w_in2[:, :width] + lax.ppermute(d_w_in2[:, width:], "tp", swap)
         d_w_out = d_w_out2[:width] + lax.ppermute(d_w_out2[width:], "tp", swap)
 
-        d_scaled = jnp.concatenate(d_normed, axis=0) * gain_f32
+        d_scaled = d_normed * gain_f32
         row_proj = jnp.mean(d_scaled * emb, axis=-1, keepdims=True)
         d_emb = (d_out.astype(f32) + inv * (d_scaled - emb * inv * inv * row_proj)).astype(bf16)
         d_emb_full = lax.all_gather(d_emb, "tp", axis=0, tiled=True)

time: 686 us -> 602 us (0.88)
  waiting for transfers between devices: 478 us -> 250 us
  Pallas kernels: 0 us -> 141 us
    pallas_call x0 -> x1, Pallas kernels: none -> 141 us  [exchange(): pl.pallas_call(functools.partial(exchange_kernel, side), out_shape=(jax.S...]
    reduce_scatter x4 -> x2, waiting for transfers between devices: 305 us -> 184 us  [scatter_plane(): lax.psum_scatter(v, 'tp', scatter_dimension=0, tiled=True, axis_index_gro...]
    all_gather x3 -> x1, waiting for transfers between devices: 99.3 us -> 0.01 us  [gather_plane(): return lax.all_gather(v, 'tp', axis=0, tiled=True, axis_index_groups=planes)]
    dot_general x12 -> x9, matrix products: 159 us -> 165 us  [dot(): lax.dot_general(a, b, (((ca,), (cb,)), ((), ())), preferred_element_type=...]
  transfers between devices with their start and end apart: 13 -> 9, of which waited for: 11 -> 4; matrix products, arithmetic and copies ran while one was open for 25% -> 25% of each run, Pallas kernels for 0% -> 24%
where the time goes in v2:
time: 602 us; the launch traced here: 593 us
  waiting for transfers between devices  250 us (42%)
  matrix products  165 us (27%)
  Pallas kernels  141 us (23%)
  between operations  14.4 us (2%)
  other arithmetic  11.6 us (2%)
  local copies, waits for them, and re-layouts  7.48 us (1%)
    reduce_scatter x2, waiting for transfers between devices, scatter_plane(): lax.psum_scatter(v, 'tp', scatter_dimension=0, tiled=True, axis_index_gro...  184 us
    dot_general x9, matrix products, dot(): lax.dot_general(a, b, (((ca,), (cb,)), ((), ())), preferred_element_type=...  165 us
    pallas_call x1, Pallas kernels, exchange(): pl.pallas_call(functools.partial(exchange_kernel, side), out_shape=(jax.S...  141 us
    all_gather x1, waiting for transfers between devices, shard_step(): d_emb_full = lax.all_gather(d_emb, 'tp', axis=0, tiled=True)  62.2 us
  transfers between devices with their start and end apart: 9, of which 4 were waited for; matrix products, arithmetic and copies ran while one was open for 25% of the time, Pallas kernels for 24%

profile of v2, /device:TPU:97, one launch (start us, length us, event | category | flops | bytes accessed | tf_op | source)
XLA Modules:
  0.0 593.0 jit_solution(13762160132450614793)
XLA Ops:
  7.2 0.1 all-gather.3.cloned.1.call-start
  7.2 2.1 collective-permute-start
  9.4 0.1 all-gather.3.cloned.1.call-update
  9.4 0.1 reduce-scatter.3.cloned.1.call-start
  9.5 0.7 collective-permute-start.1
  10.2 0.1 collective-permute-start.2
  10.3 0.7 broadcast_subtract_fusion.1
  11.0 0.0 copy-start.2
  11.1 0.0 copy-start.3
  11.1 23.9 %fusion.1 = f32[2048,2560]{1,0:T(8,128)} fusion(bf16[1600,2560]{1,0:T(8,128)(2,1)} %param.7, s32[2048]{0:T(1024)S(1)} %bitcast.27), kind=kOutput, calls=%fused_computation.5 | convolution fusion | flops 16780492800 | bytes 29171712 | tf_op jit(solution)/shard_map/dot_general | solution.py:193
  34.9 0.6 reshape.50.gain_ref
  35.6 0.1 constant_dynamic-update-slice_fusion.1
  35.7 0.1 constant_dynamic-update-slice_fusion.3
  35.8 0.1 constant_dynamic-update-slice_fusion
  35.9 0.1 constant_dynamic-update-slice_fusion.2
  36.1 1.8 copy-done.4
  37.9 0.8 copy-done.6
  38.7 26.9 %add_convert_fusion.look_ref = bf16[2048,2560]{1,0:T(8,128)(2,1)} fusion(f32[2048,2560]{1,0:T(8,128)} %fusion.1, bf16[1600,2560]{1,0:T(8,128)(2,1)} %collective-permute-done, s32[2048]{0:T(1024)S(1)} %bitcast.26), kind=kOutput, calls=%fused_computation.2 | convolution fusion | flops 16790978560 | bytes 39657472 | tf_op jit(solution)/shard_map/dot_general | solution.py:193
  65.6 140.8 %exchange.1 = (bf16[128,2560]{1,0:T(8,128)(2,1)}, bf16[2048,2560]{1,0:T(8,128)(2,1)}) custom-call(bf16[1,2560]{1,0:T(2,128)(2,1)} %reshape.50.gain_ref, bf16[2048,2560]{1,0:T(8,128)(2,1)} %add_convert_fusion.look_ref), custom_call_target="tpu_custom_call" | custom-call | flops 99999997952 | bytes 20971520 | tf_op jit(solution)/shard_map/exchange/pallas_call | solution.py:156
  206.4 13.2 %convolution_convert_fusion.1 = bf16[2048,640]{1,0:T(8,128)(2,1)} fusion(bf16[2048,2560]{1,0:T(8,128)(2,1)} %get-tuple-element.9, bf16[2560,640]{0,1:T(8,128)(2,1)} %copy-done.6), kind=kOutput, calls=%fused_computation.30 | convolution fusion | flops 6712197120 | bytes 16384000 | tf_op jit(solution)/shard_map/dot_general | solution.py:193
  219.6 13.7 %fusion.9 = bf16[2048,640]{1,0:T(8,128)(2,1)S(1)} fusion(bf16[2048,640]{1,0:T(8,128)(2,1)} %convolution_convert_fusion.1, bf16[640,2560]{1,0:T(8,128)(2,1)S(1)} %copy-done.5, bf16[2048,2560]{1,0:T(8,128)(2,1)} %all-gather.3.cloned.1.call-done), kind=kOutput, calls=%fused_computation.18 | convolution fusion | flops 6741032960 | bytes 19005440 | tf_op jit(solution)/shard_map/dot_general | solution.py:193
  233.3 1.5 copy-done.12
  234.8 11.4 %fusion.30 = f32[2048,2560]{1,0:T(8,128)} fusion(bf16[2048,640]{1,0:T(8,128)(2,1)S(1)} %fusion.9, bf16[2560,640]{0,1:T(8,128)(2,1)S(1)} %copy-done.7), kind=kOutput, calls=%fused_computation.55 | convolution fusion | flops 6710886400 | bytes 26869760 | tf_op jit(solution)/shard_map/dot_general | solution.py:193
  246.3 0.1 reduce-scatter.3.cloned.1.call-update
  246.3 0.1 all-gather.5.cloned.1.call-start
  246.4 0.6 copy-done.10
  247.0 126.4 %reduce-scatter.3.cloned.1.call-done = f32[128,2560]{1,0:T(8,128)} async-done(((f32[2048,2560]{1,0:T(8,128)}), f32[128,2560]{1,0:T(8,128)}) %reduce-scatter.3.cloned.1.call-update) | async-done | bytes 1310736 | tf_op jit(solution)/shard_map/reduce_scatter | solution.py:190
  373.4 1.7 fusion.17
  375.0 2.6 fusion.23
  377.7 0.1 all-gather.5.cloned.1.call-update
  377.7 0.1 reduce-scatter.5.cloned.1.call-start
  377.8 15.2 %fusion.28 = f32[2048,2560]{1,0:T(8,128)} fusion(bf16[640,2560]{1,0:T(8,128)(2,1)} %copy-done.4, bf16[2048,640]{1,0:T(8,128)(2,1)} %convolution_convert_fusion.1), kind=kOutput, calls=%fused_computation.54 | convolution fusion | flops 6723993600 | bytes 26869760 | tf_op jit(solution)/shard_map/dot_general | solution.py:193
  393.1 62.2 %all-gather.5.cloned.1.call-done = bf16[4096,2560]{1,0:T(8,128)(2,1)} async-done(((bf16[128,2560]{1,0:T(8,128)(2,1)}), bf16[4096,2560]{1,0:T(8,128)(2,1)}) %all-gather.5.cloned.1.call-update) | async-done | bytes 20971536 | tf_op jit(solution)/shard_map/all_gather | solution.py:239
  455.3 0.1 reduce-scatter.5.cloned.1.call-update
  455.3 11.1 %fusion.26 = f32[640,2560]{1,0:T(8,128)S(1)} fusion(bf16[2048,2560]{1,0:T(8,128)(2,1)} %all-gather.3.cloned.1.call-done, bf16[2048,640]{1,0:T(8,128)(2,1)S(1)} %copy-done.11), kind=kOutput, calls=%fused_computation.53 | convolution fusion | flops 6723993600 | bytes 19660800 | tf_op jit(solution)/shard_map/dot_general | solution.py:193
  466.4 0.2 slice.19
  466.7 0.4 collective-permute-start.4
  467.0 1.1 copy-done.13
  468.2 10.7 %fusion.31 = f32[2560,640]{0,1:T(8,128)S(1)} fusion(bf16[2048,2560]{1,0:T(8,128)(2,1)} %get-tuple-element.9, bf16[2048,640]{1,0:T(8,128)(2,1)S(1)} %copy-done.13), kind=kOutput, calls=%fused_computation.56 | convolution fusion | flops 6710886400 | bytes 19660800 | tf_op jit(solution)/shard_map/dot_general | solution.py:193
  478.9 0.2 slice.17
  479.1 0.4 collective-permute-start.3
  479.4 0.1 copy-done.8
  479.6 2.2 slice_add_fusion
  481.7 3.3 collective-permute-done.3
  485.0 2.2 slice_add_fusion.1
  487.2 38.8 %fusion = f32[1600,2560]{1,0:T(8,128)} fusion(bf16[4096,2560]{1,0:T(8,128)(2,1)} %all-gather.5.cloned.1.call-done, s32[4096]{0:T(1024)S(1)} %broadcast_subtract_fusion), kind=kOutput, calls=%fused_computation.1 | convolution fusion | flops 33560985600 | bytes 37371904 | tf_op jit(solution)/shard_map/dot_general | solution.py:193
  526.0 57.8 %reduce-scatter.5.cloned.1.call-done = f32[128,2560]{1,0:T(8,128)} async-done(((f32[2048,2560]{1,0:T(8,128)}), f32[128,2560]{1,0:T(8,128)}) %reduce-scatter.5.cloned.1.call-update) | async-done | bytes 1310736 | tf_op jit(solution)/shard_map/reduce_scatter | solution.py:190
  583.8 2.3 fusion.25
  (28 shorter events, 0.1 us)
Async XLA Ops:
  7.2 212.4 %all-gather.3.cloned.1.call-start = ((), (), s32[]{:S(2)}) async-start(), calls=%async_computation.2 | async-start | bytes 11141120 | tf_op jit(solution)/shard_map/all_gather | solution.py:187
  7.2 30.6 %collective-permute-start = (bf16[1600,2560]{1,0:T(8,128)(2,1)}, bf16[1600,2560]{1,0:T(8,128)(2,1)}, u32[]{:S(2)}, u32[]{:S(2)}) collective-permute-start(bf16[1600,2560]{1,0:T(8,128)(2,1)} %param.7), channel_id=1, source_target_pairs={{0,1},{1,0},{2,3},{3,2},{4,5},{5,4},{6,7},{7,6},{8,9},{9,8},{10,11... | collective-permute-start | bytes 24576008 | tf_op jit(solution)/shard_map/ppermute | solution.py:209
  9.4 363.9 %reduce-scatter.3.cloned.1.call-start = ((), (), s32[]{:S(2)}) async-start(), calls=%async_computation.3 | async-start | bytes 22282240 | tf_op jit(solution)/shard_map/reduce_scatter | solution.py:190
  9.5 26.3 %collective-permute-start.1 = (bf16[2560,320]{0,1:T(8,128)(2,1)}, bf16[2560,320]{0,1:T(8,128)(2,1)S(1)}, u32[]{:S(2)}, u32[]{:S(2)}) collective-permute-start(bf16[2560,320]{0,1:T(8,128)(2,1)} %param.9), channel_id=1, source_target_pairs={{0,1},{1,0},{2,3},{3,2},{4,5},{5,4},{6,7},{7,6},{8,9},{9,8},{10,11... | collective-permute-start | bytes 4915208 | tf_op jit(solution)/shard_map/ppermute | solution.py:211
  10.2 25.8 %collective-permute-start.2 = (bf16[320,2560]{1,0:T(8,128)(2,1)}, bf16[320,2560]{1,0:T(8,128)(2,1)S(1)}, u32[]{:S(2)}, u32[]{:S(2)}) collective-permute-start(bf16[320,2560]{1,0:T(8,128)(2,1)} %param.10), channel_id=1, source_target_pairs={{0,1},{1,0},{2,3},{3,2},{4,5},{5,4},{6,7},{7,6},{8,9},{9,8},{10,11... | collective-permute-start | bytes 4915208 | tf_op jit(solution)/shard_map/ppermute | solution.py:210
  11.0 23.9 %copy-start.9 = (bf16[2560]{0:T(1024)(128)(2,1)S(1)}, bf16[2560]{0:T(1024)(128)(2,1)}, u32[]{:S(2)}) copy-start(bf16[2560]{0:T(1024)(128)(2,1)} %param.8) | copy-start | bytes 15364
  11.0 24.5 %copy-start.2 = (bf16[2560,320]{0,1:T(8,128)(2,1)S(1)}, bf16[2560,320]{0,1:T(8,128)(2,1)}, u32[]{:S(2)}) copy-start(bf16[2560,320]{0,1:T(8,128)(2,1)} %param.9) | copy-start | bytes 4915204
  11.1 24.6 %copy-start.3 = (bf16[320,2560]{1,0:T(8,128)(2,1)S(1)}, bf16[320,2560]{1,0:T(8,128)(2,1)}, u32[]{:S(2)}) copy-start(bf16[320,2560]{1,0:T(8,128)(2,1)} %param.10) | copy-start | bytes 4915204
  35.9 2.8 copy-start.6
  36.1 1.8 copy-start.4
  206.4 13.2 %copy-start.5 = (bf16[640,2560]{1,0:T(8,128)(2,1)S(1)}, bf16[640,2560]{1,0:T(8,128)(2,1)}, u32[]{:S(2)}) copy-start(bf16[640,2560]{1,0:T(8,128)(2,1)} %copy-done.4) | copy-start | bytes 9830404
  219.6 15.2 %copy-start.7 = (bf16[2560,640]{0,1:T(8,128)(2,1)S(1)}, bf16[2560,640]{0,1:T(8,128)(2,1)}, u32[]{:S(2)}) copy-start(bf16[2560,640]{0,1:T(8,128)(2,1)} %copy-done.6) | copy-start | bytes 9830404
  233.3 1.5 copy-start.12
  246.3 0.7 copy-start.10
  246.3 127.1 %copy-start = (bf16[128,2560]{1,0:T(8,128)(2,1)S(1)}, bf16[128,2560]{1,0:T(8,128)(2,1)}, u32[]{:S(2)}) copy-start(bf16[128,2560]{1,0:T(8,128)(2,1)} %get-tuple-element.8) | copy-start | bytes 1966084
  246.3 128.8 %copy-start.1 = (bf16[128,2560]{1,0:T(8,128)(2,1)S(1)}, bf16[128,2560]{1,0:T(8,128)(2,1)}, u32[]{:S(2)}) copy-start(bf16[128,2560]{1,0:T(8,128)(2,1)} %param.11) | copy-start | bytes 1966084
  246.3 208.9 %all-gather.5.cloned.1.call-start = ((), (), s32[]{:S(2)}) async-start(), calls=%async_computation.4 | async-start | bytes 21626880 | tf_op jit(solution)/shard_map/all_gather | solution.py:239
  377.7 206.1 %reduce-scatter.5.cloned.1.call-start = ((), (), s32[]{:S(2)}) async-start(), calls=%async_computation.5 | async-start | bytes 22282240 | tf_op jit(solution)/shard_map/reduce_scatter | solution.py:190
  393.0 62.3 %copy-start.11 = (bf16[2048,640]{1,0:T(8,128)(2,1)S(1)}, bf16[2048,640]{1,0:T(8,128)(2,1)}, u32[]{:S(2)}) copy-start(bf16[2048,640]{1,0:T(8,128)(2,1)} %convolution_convert_fusion.1) | copy-start | bytes 7864324
  466.4 1.7 copy-start.13
  466.7 12.9 %collective-permute-start.4 = (f32[320,2560]{1,0:T(8,128)S(1)}, f32[320,2560]{1,0:T(8,128)S(1)}, u32[]{:S(2)}, u32[]{:S(2)}) collective-permute-start(f32[320,2560]{1,0:T(8,128)S(1)} %slice.19), channel_id=1, source_target_pairs={{0,1},{1,0},{2,3},{3,2},{4,5},{5,4},{6,7},{7,6},{8,9},{9,8},{10,11... | collective-permute-start | bytes 9830408 | tf_op jit(solution)/shard_map/ppermute | solution.py:234
  478.8 0.7 copy-start.8
  479.1 5.9 %collective-permute-start.3 = (f32[2560,320]{0,1:T(8,128)S(1)}, f32[2560,320]{0,1:T(8,128)S(1)}, u32[]{:S(2)}, u32[]{:S(2)}) collective-permute-start(f32[2560,320]{0,1:T(8,128)S(1)} %slice.17), channel_id=1, source_target_pairs={{0,1},{1,0},{2,3},{3,2},{4,5},{5,4},{6,7},{7,6},{8,9},{9,8},{10,11... | collective-permute-start | bytes 9830408 | tf_op jit(solution)/shard_map/ppermute | solution.py:233
Sparse Core Ops, SparseCore 0:
  10.0 89.4 all-gather.2
  246.4 126.8 reduce-scatter.2
  377.8 77.3 all-gather.4
  458.4 125.3 reduce-scatter.4
